TPU v7x, 32 devices: a whole 2x2x4 slice. The times are simulated.
32 devices in a mesh: tg: 2 (over core), pw: 16 (over z, y, x).
Axes of the slice: x: 2, y: 2, z: 4, core: 2. Of those that a mesh axis runs over, the one named last changes fastest.
Arguments:
- coeffs: float32 [2, 8192, 256], P(None, ('tg', 'pw')), may hold values from -6 to 6
- g_place: int32 [8192], P(('tg', 'pw')), may hold values from 0 to 2047, as said below
- stick_column: int32 [512], P(('tg', 'pw')), may hold values from 0 to 16383, as said below
- potential: float32 [128, 128, 128], P(None, None, ('tg', 'pw')), may hold values from -1 to 3
Outputs:
- hpsi: float32 [2, 8192, 256], P(None, ('tg', 'pw'))
Inputs may be any that keep to these rules, and one draw needn't show every extreme that they name: g_place[g] = s * 128 + z: s is a stick slot of the owner g // 256, z a frequency within 32 of zero taken modulo 128; no two plane waves of one owner share s and z; each owner uses its slots 0 up to some count between 4 and 16, every one of them, and some owner uses all 16. `stick_column`: all stick slots name different columns x * 128 + y; with x and y read as signed frequencies (taken modulo 128), x * x + y * y <= 32 ** 2.
All inputs are finite; a program needn't handle non-finite values.
Results may differ from a plain program's by a relative error of at most 0.009.
Values may be sent and summed in bfloat16 or wider, within the bound.
A program may use at most 256 MiB of HBM per device.

v0:
```python
import jax
import jax.numpy as jnp
from jax import lax
from jax.sharding import PartitionSpec as P

NR = 128
ZSPAN = 64


def phase_table(left_index, right_index, sign_value, modulus):
    product = left_index[:, None] * right_index[None, :] % modulus
    angles = 2.0 * jnp.pi / modulus * product.astype(jnp.float32)
    cosine = jnp.cos(angles)
    sine_part = sign_value * jnp.sin(angles)
    upper_row = jnp.stack([cosine, sine_part])
    lower_row = jnp.stack([-sine_part, cosine])
    return jnp.stack([upper_row, lower_row])


def box_selectors(column_order):
    half_span = ZSPAN // 2
    box_side = ZSPAN + 1
    x_index = column_order // NR
    y_index = column_order % NR
    x_box = jnp.where(x_index > NR // 2, x_index - NR, x_index) + half_span
    y_box = jnp.where(y_index > NR // 2, y_index - NR, y_index) + half_span
    cells = jnp.arange(box_side * box_side, dtype=jnp.int32)
    forward_select = (cells[:, None] == (y_box * box_side + x_box)[None, :]).astype(jnp.bfloat16)
    backward_select = (cells[:, None] == (x_box * box_side + y_box)[None, :]).astype(jnp.bfloat16)
    return (forward_select, backward_select)


def box_tables():
    box_side = ZSPAN + 1
    frequency = jnp.arange(NR, dtype=jnp.int32)
    box_freq = jnp.mod(jnp.arange(box_side, dtype=jnp.int32) - ZSPAN // 2, NR)
    ahead = phase_table(box_freq, frequency, 1.0, NR).astype(jnp.bfloat16)
    behind = phase_table(frequency, box_freq, -1.0, NR).astype(jnp.bfloat16)
    return (ahead, behind)


def one_plane(flat, volume, selectors, ahead, behind):
    forward_select, backward_select = selectors
    box_side = ZSPAN + 1
    band_count = flat.shape[2]
    lattice = jnp.stack(
        [
            jnp.dot(forward_select, flat[part_index], preferred_element_type=jnp.float32)
            .astype(jnp.bfloat16)
            .reshape(box_side, box_side, band_count)
            for part_index in range(2)
        ]
    )
    partial_value = jnp.einsum(
        "cdyk,cyxm->dkxm", ahead, lattice, preferred_element_type=jnp.float32
    ).astype(jnp.bfloat16)
    psi_field = jnp.einsum(
        "cdxr,ckxm->drkm", ahead, partial_value, preferred_element_type=jnp.float32
    )
    weighted = (psi_field * volume[None, :, :, None]).astype(jnp.bfloat16)
    reverse_half = jnp.einsum(
        "cdyq,cxym->dqxm", behind, weighted, preferred_element_type=jnp.float32
    ).astype(jnp.bfloat16)
    real_image = jnp.einsum(
        "cdxq,cyxm->dqym", behind, reverse_half, preferred_element_type=jnp.float32
    )
    boxed = real_image.astype(jnp.bfloat16).reshape(2, box_side * box_side, band_count)
    picked = jnp.stack(
        [
            jnp.einsum(
                "qs,qm->sm", backward_select, boxed[part_index], preferred_element_type=jnp.float32
            )
            for part_index in range(2)
        ]
    )
    return picked.astype(jnp.bfloat16)


def plane_pass(received, selectors, volume, ahead, behind):
    def step(carry, item):
        return carry, one_plane(item[0], item[1], selectors, ahead, behind)

    planes = (jnp.moveaxis(received, 2, 0), jnp.moveaxis(volume, 2, 0))
    return jnp.moveaxis(lax.scan(step, None, planes)[1], 0, 2)


def spread(shared, indices, slot_total):
    band_count = shared.shape[2]
    selector = (indices[:, None] == jnp.arange(slot_total * NR, dtype=jnp.int32)[None, :]).astype(
        jnp.float32
    )
    placed = jnp.einsum("gq,cgb->cqb", selector, shared, precision=lax.Precision.HIGHEST)
    return (selector, placed.reshape(2, slot_total, NR, band_count))


def ahead_sticks(placed, plane_of):
    frequency = jnp.arange(NR, dtype=jnp.int32)
    ahead_table = phase_table(frequency, plane_of, 1.0, NR)
    sticks = jnp.einsum("cszb,cdzk->dskb", placed, ahead_table, precision=lax.Precision.HIGHEST)
    return sticks.astype(jnp.bfloat16)


def finish(arrived, plane_of, selector):
    frequency = jnp.arange(NR, dtype=jnp.int32)
    return_table = phase_table(plane_of, frequency, -1.0, NR)
    spectra = jnp.einsum(
        "cszb,cdzk->dskb",
        arrived.astype(jnp.float32),
        return_table,
        precision=lax.Precision.HIGHEST,
    )
    band_count = arrived.shape[3]
    picked = jnp.einsum(
        "gq,cqb->cgb", selector, spectra.reshape(2, -1, band_count), precision=lax.Precision.HIGHEST
    )
    return picked * (1.0 / NR**3)


def body(coeffs, g_place, stick_column, potential):
    owners = lax.axis_size(("tg", "pw"))
    copies = jnp.broadcast_to(stick_column[None], (owners,) + stick_column.shape)
    columns = lax.all_to_all(
        copies, ("tg", "pw"), split_axis=0, concat_axis=0, tiled=True
    ).reshape(-1)
    ahead, behind = box_tables()
    slot_width = stick_column.shape[0]
    plane_of = jnp.arange(NR, dtype=jnp.int32)
    selector, placed = spread(coeffs, g_place, slot_width)
    sticks = ahead_sticks(placed, plane_of)
    selectors = box_selectors(columns)
    returned = plane_pass(
        lax.all_to_all(sticks, ("tg", "pw"), split_axis=2, concat_axis=1, tiled=True),
        selectors,
        potential,
        ahead,
        behind,
    )
    arrived = lax.all_to_all(returned, ("tg", "pw"), split_axis=1, concat_axis=2, tiled=True)
    return finish(arrived, plane_of, selector)


def solution(mesh):
    placed = (
        P(None, ("tg", "pw"), None),
        P(("tg", "pw")),
        P(("tg", "pw")),
        P(None, None, ("tg", "pw")),
    )
    return jax.shard_map(
        body, mesh=mesh, in_specs=placed, out_specs=P(None, ("tg", "pw"), None), check_vma=False
    )
```

profile of v0, /device:TPU:0, one launch (start us, length us, event | category | flops | bytes accessed | tf_op | source)
XLA Modules:
  0.0 544.8 jit_solution(8175627262599642719)
XLA Ops:
  1.3 7.3 %all-to-all-start.1 = ((s32[32,1,16]{2,1,0:T(1,128)}), s32[32,1,16]{2,1,0:T(1,128)S(1)}, u32[]{:S(2)}, u32[]{:S(2)}) async-start(s32[32,1,16]{2,1,0:T(1,128)} %broadcast_in_dim.6), calls=%async_computation.1 | async-start | bytes 32768 | tf_op jit(solution)/shard_map/all_to_all | solution.py:122
  12.9 3.8 fusion.51
  19.3 5.8 %all-to-all-start = ((bf16[2,16,128,256]{3,1,0,2:T(8,128)(2,1)}), bf16[2,16,128,256]{3,1,0,2:T(8,128)(2,1)S(1)}, u32[]{:S(2)}, u32[]{:S(2)}) async-start(bf16[2,16,128,256]{3,1,0,2:T(8,128)(2,1)} %copy.40), calls=%async_computation | async-start | bytes 4194304 | tf_op jit(solution)/shard_map/all_to_all | solution.py:132
  27.0 48.8 %all-to-all-done = bf16[2,16,128,256]{3,1,0,2:T(8,128)(2,1)S(1)} async-done(((bf16[2,16,128,256]{3,1,0,2:T(8,128)(2,1)}), bf16[2,16,128,256]{3,1,0,2:T(8,128)(2,1)S(1)}, u32[]{:S(2)}, u32[]{:S(2)}) %all-to-all-start) | async-done | bytes 2097184 | tf_op jit(solution)/shard_map/all_to_all | solution.py:132
  77.2 399.3 %while.11 = (s32[]{:T(128)}, bf16[4,2,512,256]{2,3,1,0:T(8,128)(2,1)}, bf16[4,2,512,256]{3,2,1,0:T(8,128)(2,1)}, bf16[2,2,65,128]{3,2,0,1:T(8,128)(2,1)S(1)}, f3...) while((s32[]{:T(128)}, ...), condition=%wide.region_1.2_spmd.clone, body=%wide.region_0.1_spmd.clone.sunk | while | flops 11064318976 | bytes 190150320 | solution.py:84
  94.5 4.9 fusion.150
  99.3 12.5 %copy.100 = bf16[2,128,65,256,1]{3,2,0,4,1:T(8,128)(2,1)} copy(bf16[2,128,65,256,1]{1,3,0,2,4:T(8,128)(2,1)} %fusion.150) | data formatting | bytes 17039360 | tf_op jit(solution)/shard_map/while/body/eval_jaxpr/convert_element_type | solution.py:56
  112.0 14.1 %fusion.151 = bf16[2,128,128,256,1]{1,3,0,2,4:T(8,128)(2,1)} fusion(f32[128,128]{0,1:T(8,128)S(1)} %copy.97, bf16[2,128,65,256,1]{3,2,0,4,1:T(8,128)(2,1)} %copy.100, bf16[2,2,65,128]{3,2,0,1:T(8,128)(2,1)S(1)} %get-tuple-element.185), kind=kOutput, calls=%fused_computation.6.clone.1 | convolution fusion | flops 2197815296 | bytes 25428992 | tf_op jit(solution)/shard_map/while/body/eval_jaxpr/cdxr,ckxm->drkm/dot_general | solution.py:57
  126.0 23.5 %copy.101 = bf16[2,128,128,256,1]{3,2,0,4,1:T(8,128)(2,1)} copy(bf16[2,128,128,256,1]{1,3,0,2,4:T(8,128)(2,1)} %fusion.151) | data formatting | bytes 33554432 | tf_op jit(solution)/shard_map/while/body/eval_jaxpr/convert_element_type | solution.py:60
  149.5 7.2 %fusion.152 = bf16[2,65,128,256,1]{3,1,0,2,4:T(8,128)(2,1)S(1)} fusion(bf16[2,128,128,256,1]{3,2,0,4,1:T(8,128)(2,1)} %copy.101, bf16[2,2,128,65]{2,3,0,1:T(8,128)(2,1)S(1)} %get-tuple-element.187), kind=kOutput, calls=%fused_computation.8.clone.1 | convolution fusion | flops 2185297920 | bytes 25363456 | tf_op jit(solution)/shard_map/while/body/eval_jaxpr/cdyq,cxym->dqxm/dot_general | solution.py:61
  162.3 4.4 squeeze.22
  185.8 3.6 fusion.149
  194.3 4.9 fusion.150
  199.1 12.5 %copy.100 = bf16[2,128,65,256,1]{3,2,0,4,1:T(8,128)(2,1)} copy(bf16[2,128,65,256,1]{1,3,0,2,4:T(8,128)(2,1)} %fusion.150) | data formatting | bytes 17039360 | tf_op jit(solution)/shard_map/while/body/eval_jaxpr/convert_element_type | solution.py:56
  211.8 14.1 %fusion.151 = bf16[2,128,128,256,1]{1,3,0,2,4:T(8,128)(2,1)} fusion(f32[128,128]{0,1:T(8,128)S(1)} %copy.97, bf16[2,128,65,256,1]{3,2,0,4,1:T(8,128)(2,1)} %copy.100, bf16[2,2,65,128]{3,2,0,1:T(8,128)(2,1)S(1)} %get-tuple-element.185), kind=kOutput, calls=%fused_computation.6.clone.1 | convolution fusion | flops 2197815296 | bytes 25428992 | tf_op jit(solution)/shard_map/while/body/eval_jaxpr/cdxr,ckxm->drkm/dot_general | solution.py:57
  225.8 23.5 %copy.101 = bf16[2,128,128,256,1]{3,2,0,4,1:T(8,128)(2,1)} copy(bf16[2,128,128,256,1]{1,3,0,2,4:T(8,128)(2,1)} %fusion.151) | data formatting | bytes 33554432 | tf_op jit(solution)/shard_map/while/body/eval_jaxpr/convert_element_type | solution.py:60
  249.3 7.2 %fusion.152 = bf16[2,65,128,256,1]{3,1,0,2,4:T(8,128)(2,1)S(1)} fusion(bf16[2,128,128,256,1]{3,2,0,4,1:T(8,128)(2,1)} %copy.101, bf16[2,2,128,65]{2,3,0,1:T(8,128)(2,1)S(1)} %get-tuple-element.187), kind=kOutput, calls=%fused_computation.8.clone.1 | convolution fusion | flops 2185297920 | bytes 25363456 | tf_op jit(solution)/shard_map/while/body/eval_jaxpr/cdyq,cxym->dqxm/dot_general | solution.py:61
  262.1 4.4 squeeze.22
  294.1 4.9 fusion.150
  298.9 12.5 %copy.100 = bf16[2,128,65,256,1]{3,2,0,4,1:T(8,128)(2,1)} copy(bf16[2,128,65,256,1]{1,3,0,2,4:T(8,128)(2,1)} %fusion.150) | data formatting | bytes 17039360 | tf_op jit(solution)/shard_map/while/body/eval_jaxpr/convert_element_type | solution.py:56
  311.6 14.1 %fusion.151 = bf16[2,128,128,256,1]{1,3,0,2,4:T(8,128)(2,1)} fusion(f32[128,128]{0,1:T(8,128)S(1)} %copy.97, bf16[2,128,65,256,1]{3,2,0,4,1:T(8,128)(2,1)} %copy.100, bf16[2,2,65,128]{3,2,0,1:T(8,128)(2,1)S(1)} %get-tuple-element.185), kind=kOutput, calls=%fused_computation.6.clone.1 | convolution fusion | flops 2197815296 | bytes 25428992 | tf_op jit(solution)/shard_map/while/body/eval_jaxpr/cdxr,ckxm->drkm/dot_general | solution.py:57
  325.6 23.5 %copy.101 = bf16[2,128,128,256,1]{3,2,0,4,1:T(8,128)(2,1)} copy(bf16[2,128,128,256,1]{1,3,0,2,4:T(8,128)(2,1)} %fusion.151) | data formatting | bytes 33554432 | tf_op jit(solution)/shard_map/while/body/eval_jaxpr/convert_element_type | solution.py:60
  349.1 7.2 %fusion.152 = bf16[2,65,128,256,1]{3,1,0,2,4:T(8,128)(2,1)S(1)} fusion(bf16[2,128,128,256,1]{3,2,0,4,1:T(8,128)(2,1)} %copy.101, bf16[2,2,128,65]{2,3,0,1:T(8,128)(2,1)S(1)} %get-tuple-element.187), kind=kOutput, calls=%fused_computation.8.clone.1 | convolution fusion | flops 2185297920 | bytes 25363456 | tf_op jit(solution)/shard_map/while/body/eval_jaxpr/cdyq,cxym->dqxm/dot_general | solution.py:61
  361.9 4.4 squeeze.22
  385.4 3.6 fusion.149
  393.9 4.9 fusion.150
  398.8 12.5 %copy.100 = bf16[2,128,65,256,1]{3,2,0,4,1:T(8,128)(2,1)} copy(bf16[2,128,65,256,1]{1,3,0,2,4:T(8,128)(2,1)} %fusion.150) | data formatting | bytes 17039360 | tf_op jit(solution)/shard_map/while/body/eval_jaxpr/convert_element_type | solution.py:56
  411.4 14.1 %fusion.151 = bf16[2,128,128,256,1]{1,3,0,2,4:T(8,128)(2,1)} fusion(f32[128,128]{0,1:T(8,128)S(1)} %copy.97, bf16[2,128,65,256,1]{3,2,0,4,1:T(8,128)(2,1)} %copy.100, bf16[2,2,65,128]{3,2,0,1:T(8,128)(2,1)S(1)} %get-tuple-element.185), kind=kOutput, calls=%fused_computation.6.clone.1 | convolution fusion | flops 2197815296 | bytes 25428992 | tf_op jit(solution)/shard_map/while/body/eval_jaxpr/cdxr,ckxm->drkm/dot_general | solution.py:57
  425.5 23.5 %copy.101 = bf16[2,128,128,256,1]{3,2,0,4,1:T(8,128)(2,1)} copy(bf16[2,128,128,256,1]{1,3,0,2,4:T(8,128)(2,1)} %fusion.151) | data formatting | bytes 33554432 | tf_op jit(solution)/shard_map/while/body/eval_jaxpr/convert_element_type | solution.py:60
  448.9 7.2 %fusion.152 = bf16[2,65,128,256,1]{3,1,0,2,4:T(8,128)(2,1)S(1)} fusion(bf16[2,128,128,256,1]{3,2,0,4,1:T(8,128)(2,1)} %copy.101, bf16[2,2,128,65]{2,3,0,1:T(8,128)(2,1)S(1)} %get-tuple-element.187), kind=kOutput, calls=%fused_computation.8.clone.1 | convolution fusion | flops 2185297920 | bytes 25363456 | tf_op jit(solution)/shard_map/while/body/eval_jaxpr/cdyq,cxym->dqxm/dot_general | solution.py:61
  461.7 4.4 squeeze.22
  480.0 52.3 %all_to_all.42 = bf16[2,512,4,256]{3,2,0,1:T(4,128)(2,1)S(1)} all-to-all(bf16[2,512,4,256]{3,2,0,1:T(4,128)(2,1)S(1)} %bitcast.207), channel_id=1, replica_groups=mesh['tg'=2,'pw'=16] {'tg','pw'}, dimensions={1} | all-to-all | bytes 4194304 | tf_op jit(solution)/shard_map/all_to_all | solution.py:138
  (111 shorter events, 153.4 us)
Async XLA Ops:
  0.0 9.5 %copy-start = (f32[2,256,256]{2,1,0:T(8,128)S(1)}, f32[2,256,256]{2,1,0:T(8,128)}, u32[]{:S(2)}) copy-start(f32[2,256,256]{2,1,0:T(8,128)} %param.6) | copy-start | bytes 1572868
  1.3 18.0 %all-to-all-start.1 = ((s32[32,1,16]{2,1,0:T(1,128)}), s32[32,1,16]{2,1,0:T(1,128)S(1)}, u32[]{:S(2)}, u32[]{:S(2)}) async-start(s32[32,1,16]{2,1,0:T(1,128)} %broadcast_in_dim.6), calls=%async_computation.1 | async-start | bytes 32768 | tf_op jit(solution)/shard_map/all_to_all | solution.py:122
  16.7 8.4 %copy-start.5 = (f32[128,128,4]{1,2,0:T(4,128)S(1)}, f32[128,128,4]{1,2,0:T(4,128)}, u32[]{:S(2)}) copy-start(f32[128,128,4]{1,2,0:T(4,128)} %param.9) | copy-start | bytes 786436
  19.3 56.4 %all-to-all-start = ((bf16[2,16,128,256]{3,1,0,2:T(8,128)(2,1)}), bf16[2,16,128,256]{3,1,0,2:T(8,128)(2,1)S(1)}, u32[]{:S(2)}, u32[]{:S(2)}) async-start(bf16[2,16,128,256]{3,1,0,2:T(8,128)(2,1)} %copy.40), calls=%async_computation | async-start | bytes 4194304 | tf_op jit(solution)/shard_map/all_to_all | solution.py:132
  92.8 1.7 copy-start.2
  192.6 1.7 copy-start.2
  292.4 1.7 copy-start.2
  392.3 1.7 copy-start.2
  532.6 5.5 %copy-start.3 = (f32[1,2,128,128]{2,3,1,0:T(8,128)S(1)}, f32[1,2,128,128]{2,3,1,0:T(8,128)}, u32[]{:S(2)}) copy-start(f32[1,2,128,128]{2,3,1,0:T(8,128)} %get-tuple-element.87) | copy-start | bytes 393220
  532.6 5.5 %copy-start.4 = (f32[1,2,128,128]{2,3,1,0:T(8,128)S(1)}, f32[1,2,128,128]{2,3,1,0:T(8,128)}, u32[]{:S(2)}) copy-start(f32[1,2,128,128]{2,3,1,0:T(8,128)} %get-tuple-element.90) | copy-start | bytes 393220
  538.2 2.0 copy-start.6
  538.2 6.6 %copy-start.1 = (f32[2,256,256]{2,1,0:T(8,128)S(1)}, f32[2,256,256]{2,1,0:T(8,128)}, u32[]{:S(2)}) copy-start(f32[2,256,256]{2,1,0:T(8,128)} %param.6) | copy-start | bytes 1572868
where the time goes:
time: 551 us; the launch traced here: 545 us
  local copies, waits for them, and re-layouts  248 us (45%)
  matrix products  176 us (32%)
  blocking collectives  52.3 us (9%)
  waiting for transfers between devices  48.8 us (9%)
  starting transfers between devices  13.2 us (2%)
  other arithmetic  6.07 us (1%)
    convert_element_type x4, local copies, waits for them, and re-layouts, one_plane(): weighted = (psi_field * volume[None, :, :, None]).astype(jnp.bfloat16)  93.8 us
    dot_general x4, matrix products, one_plane(): jnp.einsum('cdxr,ckxm->drkm', ahead, partial_value, preferred_element_typ...  56.3 us
    all_to_all x1, blocking collectives, body(): lax.all_to_all(returned, ('tg', 'pw'), split_axis=1, concat_axis=2, tiled...  52.3 us
    convert_element_type x4, local copies, waits for them, and re-layouts, one_plane(): partial_value = jnp.einsum('cdyk,cyxm->dkxm', ahead, lattice, preferred_e...  50.1 us
    all_to_all x1, waiting for transfers between devices, body(): lax.all_to_all(sticks, ('tg', 'pw'), split_axis=2, concat_axis=1, tiled=T...  48.8 us
    reshape x16, local copies, waits for them, and re-layouts, one_plane(): jnp.stack([jnp.dot(forward_select, flat[part_index], preferred_element_ty...  35.4 us
    squeeze x8, local copies, waits for them, and re-layouts, one_plane(): boxed[part_index]  30.5 us
    dot_general x4, matrix products, one_plane(): jnp.einsum('cdyq,cxym->dqxm', behind, weighted, preferred_element_type=jn...  28.7 us
  transfers between devices with their start and end apart: 2, of which 1 were waited for; matrix products, arithmetic and copies ran while one was open for 2% of the time, Pallas kernels for 0%

commit v1 on v0

v1 whole, which is shorter than its diff:
```python
import jax
import jax.numpy as jnp
import numpy as np
from jax import lax
from jax.experimental import pallas as pl
from jax.experimental.pallas import tpu as pltpu
from jax.sharding import PartitionSpec as P

NR = 128
ZSPAN = 64
HALF = ZSPAN // 2
SIDE = ZSPAN + 1
PAD = 72
PITCH = 148
WIN = 80
BLOCK = 256
GROUP = 8
STEP = 13
OWNERS = 4
AXES = ("tg", "pw")
F32 = jnp.float32
BF16 = jnp.bfloat16


def unit_tables(left, right):
    angles = 2.0 * np.pi / NR * ((left[:, None] * right[None, :]) % NR)
    return np.cos(angles), np.sin(angles)


def plane_tables():
    full = np.arange(NR)
    cosine, sine = unit_tables(full, np.arange(SIDE) - HALF)
    pad = ((0, 0), (0, PAD - SIDE))
    cosine, sine = np.pad(cosine, pad), np.pad(sine, pad)
    ahead = np.block([[cosine, -sine], [sine, cosine]])
    cos_box, sin_box = unit_tables(full - HALF, full)
    made = (
        ahead,
        ahead.T,
        np.concatenate([cos_box, sin_box], 1),
        np.concatenate([-sin_box, cos_box], 1),
    )
    return tuple(jnp.asarray(table, BF16) for table in made)


def depth_tables(copies):
    planes = NR // copies
    made = []
    for copy in range(copies):
        cosine, sine = unit_tables(np.arange(NR), np.arange(planes) + copy * planes)
        turn = np.zeros((copies, 2, NR, 2, copies, planes))
        for band in range(copies):
            turn[band, 0, :, 0, band] = cosine
            turn[band, 0, :, 1, band] = sine
            turn[band, 1, :, 0, band] = -sine
            turn[band, 1, :, 1, band] = cosine
        made.append(turn.reshape(copies * 2 * NR, 2 * NR))
    return np.stack(made)


def dot(left, right):
    return jnp.dot(left, right, preferred_element_type=F32)


def dot_nt(left, right):
    return lax.dot_general(left, right, (((1,), (1,)), ((), ())), preferred_element_type=F32)


def hot(flags):
    return flags.astype(F32).astype(BF16)


def masks(mine_ref, owner, parts, slots):
    waves = mine_ref.shape[2]
    marks = mine_ref[owner, parts:parts + 8, :].astype(F32)
    depth = lax.broadcasted_iota(jnp.int32, (NR, waves), 0).astype(F32) == marks[1:2]
    slot = lax.broadcasted_iota(jnp.int32, (slots, waves), 0).astype(F32) == marks[0:1]
    return hot(depth), slot


def permute(source, target, index_ref):
    sticks = source.shape[1]

    def one(step, carry):
        rows = pl.ds(pl.multiple_of(step * BLOCK, BLOCK), BLOCK)
        wanted = lax.broadcasted_iota(jnp.int32, (BLOCK, sticks), 0) + step * BLOCK
        choice = hot(wanted == index_ref[...])
        for part in range(2):
            for chunk in range(source.shape[2] // BLOCK):
                lanes = pl.ds(chunk * BLOCK, BLOCK)
                target[part, rows, lanes] = dot(choice, source[part, :, lanes].astype(BF16)).astype(BF16)
        return carry

    lax.fori_loop(0, sticks // BLOCK, one, 0)


def rise_kernel(mine_ref, rank_ref, depth_ref, packed_ref, loose):
    owners = mine_ref.shape[0]
    parts = mine_ref.shape[1] - 8
    slots = rank_ref.shape[1] // owners
    bands = parts // 2
    twin = depth_ref.shape[0] // (2 * NR)

    def spread(step, carry):
        placed = []
        for inner in range(OWNERS):
            owner = step * OWNERS + inner
            depth, slot = masks(mine_ref, owner, parts, slots)
            values = mine_ref[owner, :parts, :].astype(F32)
            rows = [jnp.where(slot, values[part:part + 1], 0.0) for part in range(parts)]
            placed.append(dot_nt(jnp.concatenate(rows, 0).astype(BF16), depth).astype(BF16))
        turned = []
        for inner in range(OWNERS):
            rows = []
            for pair in range(bands // twin):
                cells = []
                for band in range(twin):
                    for part in range(2):
                        at = (part * bands + pair * twin + band) * slots
                        cells.append(placed[inner][at:at + slots])
                rows.append(jnp.concatenate(cells, 1))
            turned.append(dot(jnp.concatenate(rows, 0), depth_ref[...]).astype(BF16))
        for inner in range(OWNERS):
            where = pl.ds(pl.multiple_of((step * OWNERS + inner) * slots, slots), slots)
            for part in range(2):
                for pair in range(bands // twin):
                    loose[part, where, pl.ds(pair * NR, NR)] = turned[inner][
                        pair * slots:(pair + 1) * slots, part * NR:(part + 1) * NR
                    ]
        return carry

    lax.fori_loop(0, owners // OWNERS, spread, 0)
    permute(loose, packed_ref, rank_ref)


def plane_kernel(
    near_ref, close_ref, mine_ref, order_ref, xs_ref, ys_ref, packed, volume_ref,
    ahead_ref, behind_ref, first_ref, second_ref, depth_ref,
    out_ref,
    loose, picked, mixer, work, level, rows_one, rows_two, held,
):
    owners = mine_ref.shape[0]
    parts = mine_ref.shape[1] - 8
    waves = mine_ref.shape[2]
    sticks = order_ref.shape[1]
    slots = sticks // owners
    bands = parts // 2
    twin = depth_ref.shape[1] // (2 * NR)

    def make_rows(step, carry):
        rows = pl.ds(pl.multiple_of(step * BLOCK, BLOCK), BLOCK)
        choice = hot(lax.broadcasted_iota(jnp.int32, (BLOCK, NR), 1) == xs_ref[rows, :])
        rows_one[rows, :] = dot(choice, first_ref[...]).astype(BF16)
        rows_two[rows, :] = dot(choice, second_ref[...]).astype(BF16)
        return carry

    lax.fori_loop(0, sticks // BLOCK, make_rows, 0)

    def make_mixer(step, carry):
        for inner in range(5):
            y = step * 5 + inner
            rows = pl.ds(pl.multiple_of(near_ref[y], 16), NR)
            mine = ys_ref[rows, :] == y
            mine = jnp.concatenate([mine, mine], 1)
            one = jnp.where(mine, rows_one[rows, :].astype(F32), 0.0)
            two = jnp.where(mine, rows_two[rows, :].astype(F32), 0.0)
            mixer[y] = jnp.concatenate([one.T, two.T], 1).astype(BF16)
        return carry

    lax.fori_loop(0, SIDE // 5, make_mixer, 0)

    def make_level(step, carry):
        for inner in range(8):
            rx = step * 8 + inner
            rows = [volume_ref[holder, rx].astype(F32) for holder in range(volume_ref.shape[0])]
            level[rx] = jnp.concatenate(rows * twin, 0).T
        return carry

    lax.fori_loop(0, NR // 8, make_level, 0)

    for half in range(2):
        for part in range(2):
            for row in range(SIDE, PAD):
                work[half, pl.ds(part * PAD + row, NR, stride=PITCH), :] = jnp.zeros((NR, NR), F32)

    def rows_of(step, inner):
        return pl.ds((step * GROUP + inner) * PITCH, 2 * PAD)

    def lift(step):
        data = []
        for inner in range(GROUP):
            rows = rows_of(step, inner)
            data.append(jnp.concatenate([work[0, rows, :], work[1, rows, :]], 1).astype(BF16))
        for inner in range(GROUP):
            psi = dot(ahead_ref[...], data[inner])
            here = level[step * GROUP + inner]
            here = jnp.concatenate([here, here], 1)
            here = jnp.concatenate([here, here], 0)
            held[inner] = (psi * here).astype(BF16)

    def fall():
        return [dot(behind_ref[...], held[inner]) for inner in range(GROUP)]

    def put(step, results):
        for inner in range(GROUP):
            rows = rows_of(step, inner)
            work[0, rows, :] = results[inner][:, :NR]
            work[1, rows, :] = results[inner][:, NR:]

    def tile(index, carry):
        lanes = pl.ds(pl.multiple_of(index * BLOCK, BLOCK), BLOCK)

        def stage_one(step, carry):
            results = []
            for inner in range(STEP):
                y = step * STEP + inner
                rows = pl.ds(pl.multiple_of(near_ref[y], 16), NR)
                data = jnp.concatenate([packed[0, rows, lanes], packed[1, rows, lanes]], 0)
                results.append(dot(mixer[y], data))
            for inner in range(STEP):
                y = step * STEP + inner
                for half in range(2):
                    for part in range(2):
                        work[half, pl.ds(part * PAD + y, NR, stride=PITCH), :] = results[inner][
                            part * NR:(part + 1) * NR, half * NR:(half + 1) * NR
                        ]
            return carry

        lax.fori_loop(0, SIDE // STEP, stage_one, 0)

        def stage_two(step, carry):
            results = fall()
            lift(step)
            put(step - 1, results)
            return carry

        lift(0)
        lax.fori_loop(1, NR // GROUP, stage_two, 0)
        put(NR // GROUP - 1, fall())

        def stage_three(step, carry):
            results = []
            for inner in range(STEP):
                y = step * STEP + inner
                data = [
                    jnp.concatenate(
                        [work[half, pl.ds(part * PAD + y, NR, stride=PITCH), :] for half in range(2)], 1
                    )
                    for part in range(2)
                ]
                data = jnp.concatenate(data, 0).astype(BF16)
                rows = pl.ds(pl.multiple_of(close_ref[y], 16), WIN)
                weights = jnp.concatenate([rows_one[rows, :], rows_two[rows, :]], 0)
                results.append(dot(weights, data))
            for inner in range(STEP):
                y = step * STEP + inner
                rows = pl.ds(pl.multiple_of(close_ref[y], 16), WIN)
                mine = ys_ref[rows, :] == y
                mine = jnp.concatenate([mine, mine], 1)
                for part in range(2):
                    picked[part, rows, lanes] = jnp.where(
                        mine, results[inner][part * WIN:(part + 1) * WIN], picked[part, rows, lanes]
                    )
            return carry

        lax.fori_loop(0, SIDE // STEP, stage_three, 0)
        return carry

    lax.fori_loop(0, packed.shape[2] // BLOCK, tile, 0)

    permute(picked, loose, order_ref)

    def collect(step, carry):
        total = hot(
            lax.broadcasted_iota(jnp.int32, (parts, parts * slots), 1) // slots
            == lax.broadcasted_iota(jnp.int32, (parts, parts * slots), 0)
        )
        turned = []
        for inner in range(OWNERS):
            where = pl.ds(pl.multiple_of((step * OWNERS + inner) * slots, slots), slots)
            rows = []
            for pair in range(bands // twin):
                here = pl.ds(pair * NR, NR)
                rows.append(jnp.concatenate([loose[0, where, here], loose[1, where, here]], 1))
            turned.append(dot(jnp.concatenate(rows, 0), depth_ref[...]).astype(BF16))
        waved = []
        for inner in range(OWNERS):
            depth, slot = masks(mine_ref, step * OWNERS + inner, parts, slots)
            rows = []
            for part in range(2):
                for pair in range(bands // twin):
                    for band in range(twin):
                        at = (band * 2 + part) * NR
                        rows.append(turned[inner][pair * slots:(pair + 1) * slots, at:at + NR])
            found = dot(jnp.concatenate(rows, 0), depth)
            slot = jnp.concatenate([slot] * parts, 0)
            waved.append(jnp.where(slot, found, 0.0).astype(BF16))
        for inner in range(OWNERS):
            out_ref[step * OWNERS + inner] = dot(total, waved[inner]).astype(BF16)
        return carry

    lax.fori_loop(0, owners // OWNERS, collect, 0)


def body(coeffs, g_place, stick_column, potential):
    groups = lax.axis_size("tg")
    columns = lax.axis_size("pw")
    owners = groups * columns
    waves = g_place.shape[0]
    slots = stick_column.shape[0]
    bands = coeffs.shape[2] // columns
    sticks = owners * slots
    parts = 2 * bands

    local = potential.transpose(0, 2, 1).astype(BF16)[None]
    volume = lax.all_gather(local, "pw", axis=0, tiled=True)

    sent = coeffs.astype(BF16).transpose(2, 0, 1).reshape(columns, bands, 2, waves)
    sent = sent.transpose(0, 2, 1, 3).reshape(columns, parts, waves)
    marks = jnp.stack(
        [
            g_place // NR,
            g_place % NR,
            jnp.pad(stick_column // NR, (0, waves - slots)),
            jnp.pad(stick_column % NR, (0, waves - slots)),
        ]
    )
    marks = jnp.pad(marks, ((0, 4), (0, 0))).astype(BF16)
    marks = jnp.broadcast_to(marks[None], (columns, 8, waves))
    sent = jnp.concatenate([sent, marks], 1)
    sent = jnp.broadcast_to(sent[None], (groups,) + sent.shape).reshape(owners, parts + 8, waves)
    mine = lax.all_to_all(sent, AXES, split_axis=0, concat_axis=0, tiled=True)

    sites = mine[:, parts + 2:parts + 4, :slots].astype(F32).astype(jnp.int32)
    xs = jnp.bitwise_and(sites[:, 0].reshape(sticks) + HALF, NR - 1)
    ys = jnp.bitwise_and(sites[:, 1].reshape(sticks) + HALF, NR - 1)
    key = ys * NR + xs
    rank = jnp.sum((key[None, :] < key[:, None]).astype(jnp.int32), 1)
    spot = jnp.arange(sticks, dtype=jnp.int32)
    hit = rank[None, :] == spot[:, None]
    order = jnp.sum(jnp.where(hit, spot[None, :], 0), 1)
    sorted_key = jnp.sum(jnp.where(hit, key[None, :], 0), 1)
    wide = jnp.broadcast_to(sorted_key[:, None], (sticks, NR))
    starts = jnp.sum((ys[None, :] < jnp.arange(SIDE)[:, None]).astype(jnp.int32), 1) // 16 * 16
    near = jnp.minimum(starts, sticks - NR)
    close = jnp.minimum(starts, sticks - WIN)

    depth = depth_tables(groups)
    turn = lax.axis_index("tg")
    depth_ahead = jnp.asarray(depth, BF16)[turn]
    depth_behind = jnp.asarray(depth.transpose(0, 2, 1), BF16)[turn]

    smem = pl.BlockSpec(memory_space=pltpu.SMEM)
    vmem = pl.BlockSpec(memory_space=pltpu.VMEM)
    lanes = bands * (NR // groups)
    packed = pl.pallas_call(
        rise_kernel,
        out_shape=jax.ShapeDtypeStruct((2, sticks, lanes), BF16),
        in_specs=[vmem] * 3,
        out_specs=vmem,
        scratch_shapes=[pltpu.VMEM((2, sticks, lanes), BF16)],
        compiler_params=pltpu.CompilerParams(vmem_limit_bytes=48 * 2**20),
        cost_estimate=pl.CostEstimate(flops=2 * 10**10, bytes_accessed=4 * 2**20, transcendentals=0),
        name="rise",
    )(mine, rank[None, :], depth_ahead)

    made = pl.pallas_call(
        plane_kernel,
        out_shape=jax.ShapeDtypeStruct((owners, parts, waves), BF16),
        in_specs=[smem, smem] + [vmem] * 11,
        out_specs=vmem,
        scratch_shapes=[
            pltpu.VMEM((2, sticks, lanes), BF16),
            pltpu.VMEM((2, sticks, lanes), F32),
            pltpu.VMEM((SIDE, 2 * NR, 2 * NR), BF16),
            pltpu.VMEM((2, NR * PITCH, NR), F32),
            pltpu.VMEM((NR, NR, NR), F32),
            pltpu.VMEM((sticks, 2 * NR), BF16),
            pltpu.VMEM((sticks, 2 * NR), BF16),
            pltpu.VMEM((GROUP, 2 * NR, 2 * NR), BF16),
        ],
        compiler_params=pltpu.CompilerParams(vmem_limit_bytes=60 * 2**20),
        cost_estimate=pl.CostEstimate(flops=8 * 10**10, bytes_accessed=8 * 2**20, transcendentals=0),
        name="planes",
    )(
        near, close, mine, order[None, :],
        jnp.bitwise_and(wide, NR - 1), wide // NR, packed, volume, *plane_tables(), depth_behind,
    )

    back = lax.all_to_all(made, AXES, split_axis=0, concat_axis=0, tiled=True)
    back = jnp.sum(back.reshape(groups, columns, 2, bands, waves).astype(F32), 0)
    back = back.transpose(1, 3, 0, 2).reshape(2, waves, columns * bands)
    return back * (1.0 / NR**3)


def solution(mesh):
    placed = (P(None, AXES, None), P(AXES), P(AXES), P(None, None, AXES))
    return jax.shard_map(
        body, mesh=mesh, in_specs=placed, out_specs=P(None, AXES, None), check_vma=False
    )
```

time: 551 us -> 197 us (0.36); the launches traced: 545 us -> 197 us
  local copies, waits for them, and re-layouts: 248 us -> 6.26 us
  matrix products: 176 us -> 0 us
  Pallas kernels: 0 us -> 91.4 us
  blocking collectives: 52.3 us -> 20.2 us
  between operations: 0.24 us -> 13.6 us
  starting transfers between devices: 13.2 us -> 7.37 us
    dot_general x36 -> x0, matrix products: 176 us -> none  [the longest x4 56.3 us: one_plane(): jnp.einsum('cdxr,ckxm->drkm', ahead, partial_value, preferred_element_typ...]
    convert_element_type x9 -> x0, local copies, waits for them, and re-layouts: 146 us -> none  [the longest x4 93.8 us: one_plane(): weighted = (psi_field * volume[None, :, :, None]).astype(jnp.bfloat16)]
    pallas_call x0 -> x2, Pallas kernels: none -> 91.4 us  [the longest x1 85.2 us: body(): pl.pallas_call(plane_kernel, out_shape=jax.ShapeDtypeStruct((owners, part...]
    reshape x17 -> x0, local copies, waits for them, and re-layouts: 35.5 us -> none  [the longest x16 35.4 us: one_plane(): jnp.stack([jnp.dot(forward_select, flat[part_index], preferred_element_ty...]
    all_gather x0 -> x1, waiting for transfers between devices: none -> 33.9 us  [body(): volume = lax.all_gather(local, 'pw', axis=0, tiled=True)]
    all_to_all x1, blocking collectives: 52.3 us -> 20.2 us  [body(): back = lax.all_to_all(made, AXES, split_axis=0, concat_axis=0, tiled=True)]
    all_to_all x2 -> x1, waiting for transfers between devices: 48.8 us -> 18.6 us  [body(): mine = lax.all_to_all(sent, AXES, split_axis=0, concat_axis=0, tiled=True)]
    squeeze x8 -> x2, local copies, waits for them, and re-layouts: 30.5 us -> 0.78 us  [the longest x1 0.75 us: body(): depth_behind = jnp.asarray(depth.transpose(0, 2, 1), BF16)[turn]]
  transfers between devices with their start and end apart: 2 -> 2, of which waited for: 1 -> 2; matrix products, arithmetic and copies ran while one was open for 2% -> 3% of each run, Pallas kernels for 0% -> 3%
where the time goes in v1:
time: 197 us
  Pallas kernels  91.4 us (46%)
  waiting for transfers between devices  52.5 us (27%)
  blocking collectives  20.2 us (10%)
  between operations  13.6 us (7%)
  starting transfers between devices  7.37 us (4%)
  local copies, waits for them, and re-layouts  6.26 us (3%)
  other arithmetic  5.79 us (3%)
    pallas_call x1, Pallas kernels, body(): pl.pallas_call(plane_kernel, out_shape=jax.ShapeDtypeStruct((owners, part...  85.2 us
    all_gather x1, waiting for transfers between devices, body(): volume = lax.all_gather(local, 'pw', axis=0, tiled=True)  33.9 us
    all_to_all x1, blocking collectives, body(): back = lax.all_to_all(made, AXES, split_axis=0, concat_axis=0, tiled=True)  20.2 us
    all_to_all x1, waiting for transfers between devices, body(): mine = lax.all_to_all(sent, AXES, split_axis=0, concat_axis=0, tiled=True)  18.6 us
    all_to_all x1, starting transfers between devices, body(): mine = lax.all_to_all(sent, AXES, split_axis=0, concat_axis=0, tiled=True)  7.33 us
    pallas_call x1, Pallas kernels, body(): pl.pallas_call(rise_kernel, out_shape=jax.ShapeDtypeStruct((2, sticks, la...  6.22 us
  transfers between devices with their start and end apart: 2, of which 2 were waited for; matrix products, arithmetic and copies ran while one was open for 3% of the time, Pallas kernels for 3%

profile of v1, /device:TPU:0, one launch (start us, length us, event | category | flops | bytes accessed | tf_op | source)
XLA Modules:
  0.0 197.2 jit_solution(9271861876834776179)
XLA Ops:
  6.5 0.7 fusion.14
  7.2 0.7 fusion.17
  8.0 0.0 copy-start.2
  8.0 1.2 copy.18
  9.2 0.0 copy-start.4
  9.2 0.0 copy-start.3
  9.3 0.9 broadcast_in_dim.58
  10.2 7.3 %all-to-all-start = ((bf16[32,40,256]{2,1,0:T(8,128)(2,1)}), bf16[32,40,256]{2,1,0:T(8,128)(2,1)S(1)}, u32[]{:S(2)}, u32[]{:S(2)}) async-start(bf16[32,40,256]{2,1,0:T(8,128)(2,1)} %bitcast.4), calls=%async_computation | async-start | bytes 1310720 | tf_op jit(solution)/shard_map/all_to_all | solution.py:332
  17.5 0.0 all-gather.3.cloned.1.call-start
  17.6 0.7 convert_bitcast_fusion
  18.3 0.0 all-gather.3.cloned.1.call-update
  18.4 0.8 dynamic-slice_bitcast_fusion.depth_ref
  19.1 18.6 %all-to-all-done.mine_ref = bf16[32,40,256]{2,1,0:T(8,128)(2,1)S(1)} async-done(((bf16[32,40,256]{2,1,0:T(8,128)(2,1)}), bf16[32,40,256]{2,1,0:T(8,128)(2,1)S(1)}, u32[]{:S(2)}, u32[]{:S(2)}) %all-to-all-start) | async-done | bytes 655392 | tf_op jit(solution)/shard_map/all_to_all | solution.py:332
  37.7 0.1 fusion.1
  37.9 0.1 and.75
  37.9 0.1 and.72
  38.0 0.1 convert_reduce_fusion.2
  38.2 0.3 convert_reduce_fusion.1
  38.4 1.0 select_reduce_fusion
  39.4 0.5 broadcast_minimum_fusion
  39.9 0.6 broadcast_minimum_fusion.1.near_ref
  40.5 1.0 broadcast_select_fusion.ys_ref
  41.5 6.2 %rise.1.packed = bf16[2,512,1024]{2,1,0:T(8,128)(2,1)S(1)} custom-call(bf16[32,40,256]{2,1,0:T(8,128)(2,1)S(1)} %all-to-all-done.mine_ref, s32[1,512]{1,0:T(1,128)S(1)} %bitcast.21, bf16[512,256]{1,0:T(8,128)(2,1)S(1)} %dynamic-slice_bitcast_fusion.1.depth_ref), custom_call_target="tpu_custom_call" | custom-call | flops 20000000000 | bytes 4194304 | tf_op jit(solution)/shard_map/rise/pallas_call | solution.py:356
  47.7 0.0 copy-done
  47.7 0.0 copy-start.1
  47.7 1.3 copy-done.1
  49.0 33.9 %all-gather.3.cloned.1.call-done = bf16[2048,4,128]{2,1,0:T(4,128)(2,1)} async-done(((bf16[128,4,128]{2,1,0:T(4,128)(2,1)}), bf16[2048,4,128]{2,1,0:T(4,128)(2,1)}) %all-gather.3.cloned.1.call-update) | async-done | bytes 2097168 | tf_op jit(solution)/shard_map/all_gather | solution.py:316
  82.9 0.8 broadcast_in_dim.62.xs_ref
  83.8 85.2 %planes.1 = bf16[32,32,256]{2,1,0:T(8,128)(2,1)} custom-call(s32[65]{0:T(128)} %broadcast_minimum_fusion.1.near_ref, s32[65]{0:T(128)} %get-tuple-element.9.close_ref, bf16[32,40,256]{2,1,0:T(8,128)(2,1)} %copy-done, s32[1,512]{1,0:T(1,128)} %bitcast.26, s32[512,128]{1,0:T(8,128)} %broadcast_in_dim.62.xs_ref, s32[512,128]{1,0:T(8,128)} %broadcast_select_fusion.ys_ref, ...), custom_call_target="tpu_custom_call" | custom-call | flops 80000000000 | bytes 8388608 | tf_op jit(solution)/shard_map/planes/pallas_call | solution.py:367
  168.9 20.2 %all_to_all.10 = bf16[32,32,256]{2,1,0:T(8,128)(2,1)S(1)} all-to-all(bf16[32,32,256]{2,1,0:T(8,128)(2,1)} %planes.1), channel_id=1, replica_groups=mesh['tg'=2,'pw'=16] {'tg','pw'}, dimensions={0} | all-to-all | bytes 1048576 | tf_op jit(solution)/shard_map/all_to_all | solution.py:390
  189.1 0.1 convert_reduce_fusion
  189.3 1.0 copy.21
  (21 shorter events, 0.3 us)
Async XLA Ops:
  8.0 9.6 %copy-start.2 = (f32[128,128,4]{1,2,0:T(4,128)S(1)}, f32[128,128,4]{1,2,0:T(4,128)}, u32[]{:S(2)}) copy-start(f32[128,128,4]{1,2,0:T(4,128)} %param.13) | copy-start | bytes 786436
  9.2 9.1 %copy-start.4 = (bf16[2,512,256]{2,1,0:T(8,128)(2,1)S(1)}, bf16[2,512,256]{2,1,0:T(8,128)(2,1)}, u32[]{:S(2)}) copy-start(bf16[2,512,256]{2,1,0:T(8,128)(2,1)} %constant.105.clone) | copy-start | bytes 1572868
  9.2 9.1 %copy-start.3 = (bf16[2,256,512]{2,1,0:T(8,128)(2,1)S(1)}, bf16[2,256,512]{2,1,0:T(8,128)(2,1)}, u32[]{:S(2)}) copy-start(bf16[2,256,512]{2,1,0:T(8,128)(2,1)} %constant.106.clone) | copy-start | bytes 1572868
  10.2 27.5 %all-to-all-start = ((bf16[32,40,256]{2,1,0:T(8,128)(2,1)}), bf16[32,40,256]{2,1,0:T(8,128)(2,1)S(1)}, u32[]{:S(2)}, u32[]{:S(2)}) async-start(bf16[32,40,256]{2,1,0:T(8,128)(2,1)} %bitcast.4), calls=%async_computation | async-start | bytes 1310720 | tf_op jit(solution)/shard_map/all_to_all | solution.py:332
  17.5 65.4 %all-gather.3.cloned.1.call-start = ((), (), s32[]{:S(2)}) async-start(), calls=%async_computation.2 | async-start | bytes 2228224 | tf_op jit(solution)/shard_map/all_gather | solution.py:316
  37.7 10.0 %copy-start = (bf16[32,40,256]{2,1,0:T(8,128)(2,1)}, bf16[32,40,256]{2,1,0:T(8,128)(2,1)S(1)}, u32[]{:S(2)}) copy-start(bf16[32,40,256]{2,1,0:T(8,128)(2,1)S(1)} %all-to-all-done.mine_ref) | copy-start | bytes 1966084
  47.7 1.3 copy-start.1
Sparse Core Ops, SparseCore 0:
  21.1 61.7 all-gather.2

commit v2 on v1

--- a/solution.py
+++ b/solution.py
@@ -5,6 +5,7 @@
 from jax.experimental import pallas as pl
 from jax.experimental.pallas import tpu as pltpu
 from jax.sharding import PartitionSpec as P
+
 
 NR = 128
 ZSPAN = 64
@@ -14,7 +15,6 @@
 PITCH = 148
 WIN = 80
 BLOCK = 256
-GROUP = 8
 STEP = 13
 OWNERS = 4
 AXES = ("tg", "pw")
@@ -134,18 +134,18 @@
 
 
 def plane_kernel(
-    near_ref, close_ref, mine_ref, order_ref, xs_ref, ys_ref, packed, volume_ref,
+    near_ref, close_ref, apart_ref, mine_ref, order_ref, xs_ref, ys_ref, packed, volume_ref,
     ahead_ref, behind_ref, first_ref, second_ref, depth_ref,
     out_ref,
     loose, picked, mixer, work, level, rows_one, rows_two, held,
 ):
     owners = mine_ref.shape[0]
     parts = mine_ref.shape[1] - 8
-    waves = mine_ref.shape[2]
     sticks = order_ref.shape[1]
     slots = sticks // owners
     bands = parts // 2
     twin = depth_ref.shape[1] // (2 * NR)
+    group = held.shape[0]
 
     def make_rows(step, carry):
         rows = pl.ds(pl.multiple_of(step * BLOCK, BLOCK), BLOCK)
@@ -172,7 +172,7 @@
     def make_level(step, carry):
         for inner in range(8):
             rx = step * 8 + inner
-            rows = [volume_ref[holder, rx].astype(F32) for holder in range(volume_ref.shape[0])]
+            rows = [volume_ref[apart_ref[holder], rx].astype(F32) for holder in range(volume_ref.shape[0])]
             level[rx] = jnp.concatenate(rows * twin, 0).T
         return carry
 
@@ -181,31 +181,31 @@
     for half in range(2):
         for part in range(2):
             for row in range(SIDE, PAD):
-                work[half, pl.ds(part * PAD + row, NR, stride=PITCH), :] = jnp.zeros((NR, NR), F32)
-
-    def rows_of(step, inner):
-        return pl.ds((step * GROUP + inner) * PITCH, 2 * PAD)
+                work[half, pl.ds(part * PAD + row + 2 * half, NR, stride=PITCH), :] = jnp.zeros((NR, NR), F32)
+
+    def rows_of(step, inner, half):
+        return pl.ds((step * group + inner) * PITCH + 2 * half, 2 * PAD)
 
     def lift(step):
         data = []
-        for inner in range(GROUP):
-            rows = rows_of(step, inner)
-            data.append(jnp.concatenate([work[0, rows, :], work[1, rows, :]], 1).astype(BF16))
-        for inner in range(GROUP):
+        for inner in range(group):
+            data.append(
+                jnp.concatenate([work[half, rows_of(step, inner, half), :] for half in range(2)], 1).astype(BF16)
+            )
+        for inner in range(group):
             psi = dot(ahead_ref[...], data[inner])
-            here = level[step * GROUP + inner]
+            here = level[step * group + inner]
             here = jnp.concatenate([here, here], 1)
             here = jnp.concatenate([here, here], 0)
             held[inner] = (psi * here).astype(BF16)
 
     def fall():
-        return [dot(behind_ref[...], held[inner]) for inner in range(GROUP)]
+        return [dot(behind_ref[...], held[inner]) for inner in range(group)]
 
     def put(step, results):
-        for inner in range(GROUP):
-            rows = rows_of(step, inner)
-            work[0, rows, :] = results[inner][:, :NR]
-            work[1, rows, :] = results[inner][:, NR:]
+        for inner in range(group):
+            for half in range(2):
+                work[half, rows_of(step, inner, half), :] = results[inner][:, half * NR:(half + 1) * NR]
 
     def tile(index, carry):
         lanes = pl.ds(pl.multiple_of(index * BLOCK, BLOCK), BLOCK)
@@ -221,7 +221,7 @@
                 y = step * STEP + inner
                 for half in range(2):
                     for part in range(2):
-                        work[half, pl.ds(part * PAD + y, NR, stride=PITCH), :] = results[inner][
+                        work[half, pl.ds(part * PAD + y + 2 * half, NR, stride=PITCH), :] = results[inner][
                             part * NR:(part + 1) * NR, half * NR:(half + 1) * NR
                         ]
             return carry
@@ -235,8 +235,8 @@
             return carry
 
         lift(0)
-        lax.fori_loop(1, NR // GROUP, stage_two, 0)
-        put(NR // GROUP - 1, fall())
+        lax.fori_loop(1, NR // group, stage_two, 0)
+        put(NR // group - 1, fall())
 
         def stage_three(step, carry):
             results = []
@@ -244,7 +244,7 @@
                 y = step * STEP + inner
                 data = [
                     jnp.concatenate(
-                        [work[half, pl.ds(part * PAD + y, NR, stride=PITCH), :] for half in range(2)], 1
+                        [work[half, pl.ds(part * PAD + y + 2 * half, NR, stride=PITCH), :] for half in range(2)], 1
                     )
                     for part in range(2)
                 ]
@@ -258,8 +258,10 @@
                 mine = ys_ref[rows, :] == y
                 mine = jnp.concatenate([mine, mine], 1)
                 for part in range(2):
-                    picked[part, rows, lanes] = jnp.where(
-                        mine, results[inner][part * WIN:(part + 1) * WIN], picked[part, rows, lanes]
+                    pltpu.store(
+                        picked.at[part, rows, lanes],
+                        results[inner][part * WIN:(part + 1) * WIN],
+                        mask=mine,
                     )
             return carry
 
@@ -302,6 +304,61 @@
     lax.fori_loop(0, owners // OWNERS, collect, 0)
 
 
+def return_kernel(made_ref, back_ref, arrived, total, twin_send, twin_recv, send_sem, recv_sem):
+    columns = back_ref.shape[0]
+    turn = lax.axis_index("tg")
+    here = lax.axis_index("pw")
+
+    swap = pltpu.make_async_remote_copy(
+        src_ref=made_ref.at[pl.ds(columns, columns)],
+        dst_ref=arrived,
+        send_sem=twin_send,
+        recv_sem=twin_recv,
+        device_id=(1 - turn, here),
+        device_id_type=pl.DeviceIdType.MESH,
+    )
+    swap.start()
+    swap.wait()
+
+    def add(at, carry):
+        total[at] = (made_ref[at].astype(F32) + arrived[at].astype(F32)).astype(BF16)
+        return carry
+
+    lax.fori_loop(0, columns, add, 0)
+
+    def copy(shift):
+        peer = lax.rem(here + shift, columns)
+        return pltpu.make_async_remote_copy(
+            src_ref=total.at[peer],
+            dst_ref=back_ref.at[here],
+            send_sem=send_sem.at[shift],
+            recv_sem=recv_sem.at[shift],
+            device_id=(turn, peer),
+            device_id_type=pl.DeviceIdType.MESH,
+        )
+
+    def push(shift, carry):
+        copy(shift).start()
+        return carry
+
+    lax.fori_loop(1, columns, push, 0)
+    back_ref[here] = total[here]
+
+    def finish(shift, carry):
+        copy(shift).wait_send()
+        pltpu.make_async_remote_copy(
+            src_ref=total.at[here],
+            dst_ref=back_ref.at[lax.rem(here - shift + columns, columns)],
+            send_sem=send_sem.at[shift],
+            recv_sem=recv_sem.at[shift],
+            device_id=(turn, here),
+            device_id_type=pl.DeviceIdType.MESH,
+        ).wait_recv()
+        return carry
+
+    lax.fori_loop(1, columns, finish, 0)
+
+
 def body(coeffs, g_place, stick_column, potential):
     groups = lax.axis_size("tg")
     columns = lax.axis_size("pw")
@@ -312,8 +369,18 @@
     sticks = owners * slots
     parts = 2 * bands
 
+    minor = 1
+    while minor * minor < columns:
+        minor *= 2
+    major = columns // minor
+
+    def swap(value, axis, shift):
+        size = lax.axis_size(axis)
+        return lax.ppermute(value, axis, [(at, at ^ shift) for at in range(size)])
+
     local = potential.transpose(0, 2, 1).astype(BF16)[None]
-    volume = lax.all_gather(local, "pw", axis=0, tiled=True)
+    column = [local] + [swap(local, "pw", at * minor) for at in range(1, major)]
+    column = jnp.concatenate(column)
 
     sent = coeffs.astype(BF16).transpose(2, 0, 1).reshape(columns, bands, 2, waves)
     sent = sent.transpose(0, 2, 1, 3).reshape(columns, parts, waves)
@@ -328,8 +395,13 @@
     marks = jnp.pad(marks, ((0, 4), (0, 0))).astype(BF16)
     marks = jnp.broadcast_to(marks[None], (columns, 8, waves))
     sent = jnp.concatenate([sent, marks], 1)
-    sent = jnp.broadcast_to(sent[None], (groups,) + sent.shape).reshape(owners, parts + 8, waves)
-    mine = lax.all_to_all(sent, AXES, split_axis=0, concat_axis=0, tiled=True)
+    others = [swap(column, "pw", at) for at in range(1, minor)]
+    apart = jnp.bitwise_xor(jnp.arange(columns, dtype=jnp.int32), lax.axis_index("pw"))
+    apart = apart % minor * major + apart // minor
+
+    mine = lax.all_to_all(sent, "pw", split_axis=0, concat_axis=0, tiled=True)
+    other = [swap(mine, "tg", at) for at in range(1, groups)]
+    mine = jnp.concatenate([mine] + other)
 
     sites = mine[:, parts + 2:parts + 4, :slots].astype(F32).astype(jnp.int32)
     xs = jnp.bitwise_and(sites[:, 0].reshape(sticks) + HALF, NR - 1)
@@ -363,34 +435,51 @@
         cost_estimate=pl.CostEstimate(flops=2 * 10**10, bytes_accessed=4 * 2**20, transcendentals=0),
         name="rise",
     )(mine, rank[None, :], depth_ahead)
+    packed, others = lax.optimization_barrier((packed, others))
+    volume = jnp.concatenate([column] + others)
 
     made = pl.pallas_call(
         plane_kernel,
         out_shape=jax.ShapeDtypeStruct((owners, parts, waves), BF16),
-        in_specs=[smem, smem] + [vmem] * 11,
+        in_specs=[smem, smem, smem] + [vmem] * 11,
         out_specs=vmem,
         scratch_shapes=[
             pltpu.VMEM((2, sticks, lanes), BF16),
             pltpu.VMEM((2, sticks, lanes), F32),
             pltpu.VMEM((SIDE, 2 * NR, 2 * NR), BF16),
-            pltpu.VMEM((2, NR * PITCH, NR), F32),
+            pltpu.VMEM((2, NR * PITCH + 8, NR), F32),
             pltpu.VMEM((NR, NR, NR), F32),
             pltpu.VMEM((sticks, 2 * NR), BF16),
             pltpu.VMEM((sticks, 2 * NR), BF16),
-            pltpu.VMEM((GROUP, 2 * NR, 2 * NR), BF16),
+            pltpu.VMEM((32 if sticks <= 1024 else 8, 2 * NR, 2 * NR), BF16),
         ],
         compiler_params=pltpu.CompilerParams(vmem_limit_bytes=60 * 2**20),
         cost_estimate=pl.CostEstimate(flops=8 * 10**10, bytes_accessed=8 * 2**20, transcendentals=0),
         name="planes",
     )(
-        near, close, mine, order[None, :],
+        near, close, apart, mine, order[None, :],
         jnp.bitwise_and(wide, NR - 1), wide // NR, packed, volume, *plane_tables(), depth_behind,
     )
 
-    back = lax.all_to_all(made, AXES, split_axis=0, concat_axis=0, tiled=True)
-    back = jnp.sum(back.reshape(groups, columns, 2, bands, waves).astype(F32), 0)
-    back = back.transpose(1, 3, 0, 2).reshape(2, waves, columns * bands)
-    return back * (1.0 / NR**3)
+    assert groups == 2
+    back = pl.pallas_call(
+        return_kernel,
+        out_shape=jax.ShapeDtypeStruct((columns, parts, waves), BF16),
+        in_specs=[vmem],
+        out_specs=vmem,
+        scratch_shapes=[
+            pltpu.VMEM((columns, parts, waves), BF16),
+            pltpu.VMEM((columns, parts, waves), BF16),
+            pltpu.SemaphoreType.DMA,
+            pltpu.SemaphoreType.DMA,
+            pltpu.SemaphoreType.DMA((columns,)),
+            pltpu.SemaphoreType.DMA((columns,)),
+        ],
+        compiler_params=pltpu.CompilerParams(vmem_limit_bytes=16 * 2**20, has_side_effects=True),
+        name="give_back",
+    )(made)
+    back = back.reshape(columns, 2, bands, waves).transpose(1, 3, 0, 2)
+    return back.reshape(2, waves, columns * bands).astype(F32) * (1.0 / NR**3)
 
 
 def solution(mesh):

time: 197 us -> 156 us (0.79)
  waiting for transfers between devices: 52.5 us -> 21.2 us
  blocking collectives: 20.2 us -> 0 us
  between operations: 13.6 us -> 0.2 us
  starting transfers between devices: 7.37 us -> 16.3 us
  Pallas kernels: 91.4 us -> 98.7 us
  local copies, waits for them, and re-layouts: 6.26 us -> 11.4 us
    all_gather x1 -> x0, waiting for transfers between devices: 33.9 us -> none  [body(): volume = lax.all_gather(local, 'pw', axis=0, tiled=True)]
    ppermute x0 -> x7, waiting for transfers between devices: none -> 21.2 us  [swap(): return lax.ppermute(value, axis, [(at, at ^ shift) for at in range(size)])]
    all_to_all x1 -> x0, blocking collectives: 20.2 us -> none  [body(): back = lax.all_to_all(made, AXES, split_axis=0, concat_axis=0, tiled=True)]
    all_to_all x1, waiting for transfers between devices: 18.6 us -> 0.01 us  [body(): mine = lax.all_to_all(sent, 'pw', split_axis=0, concat_axis=0, tiled=True)]
    pallas_call x0 -> x1, Pallas kernels: none -> 15.7 us  [body(): pl.pallas_call(return_kernel, out_shape=jax.ShapeDtypeStruct((columns, pa...]
    pallas_call x1, Pallas kernels: 85.2 us -> 76.8 us  [body(): pl.pallas_call(plane_kernel, out_shape=jax.ShapeDtypeStruct((owners, part...]
    ppermute x0 -> x7, starting transfers between devices: none -> 7.94 us  [swap(): return lax.ppermute(value, axis, [(at, at ^ shift) for at in range(size)])]
    unnamed x11 -> x19, local copies, waits for them, and re-layouts: 2.53 us -> 7.6 us
  transfers between devices with their start and end apart: 2 -> 8, of which waited for: 2 -> 4; matrix products, arithmetic and copies ran while one was open for 3% -> 4% of each run, Pallas kernels for 3% -> 4%
where the time goes in v2:
time: 156 us; the launch traced here: 155 us
  Pallas kernels  98.7 us (63%)
  waiting for transfers between devices  21.2 us (14%)
  starting transfers between devices  16.3 us (10%)
  local copies, waits for them, and re-layouts  11.4 us (7%)
  other arithmetic  7.61 us (5%)
    pallas_call x1, Pallas kernels, body(): pl.pallas_call(plane_kernel, out_shape=jax.ShapeDtypeStruct((owners, part...  76.8 us
    ppermute x7, waiting for transfers between devices, swap(): return lax.ppermute(value, axis, [(at, at ^ shift) for at in range(size)])  21.2 us
    pallas_call x1, Pallas kernels, body(): pl.pallas_call(return_kernel, out_shape=jax.ShapeDtypeStruct((columns, pa...  15.7 us
    all_to_all x1, starting transfers between devices, body(): mine = lax.all_to_all(sent, 'pw', split_axis=0, concat_axis=0, tiled=True)  8.34 us
    ppermute x7, starting transfers between devices, swap(): return lax.ppermute(value, axis, [(at, at ^ shift) for at in range(size)])  7.94 us
    unnamed x19, local copies, waits for them, and re-layouts  7.6 us
    pallas_call x1, Pallas kernels, body(): pl.pallas_call(rise_kernel, out_shape=jax.ShapeDtypeStruct((2, sticks, la...  6.22 us
  transfers between devices with their start and end apart: 8, of which 4 were waited for; matrix products, arithmetic and copies ran while one was open for 4% of the time, Pallas kernels for 4%

profile of v2, /device:TPU:0, one launch (start us, length us, event | category | flops | bytes accessed | tf_op | source)
XLA Modules:
  0.0 155.4 jit_solution(11246238183543817088)
XLA Ops:
  0.0 0.8 fusion.19
  0.8 0.7 fusion.14
  1.5 1.2 copy.17
  2.8 0.7 pad_maximum_fusion.1
  3.5 8.3 %all-to-all-start = ((bf16[16,40,256]{2,1,0:T(8,128)(2,1)}), bf16[16,40,256]{2,1,0:T(8,128)(2,1)S(1)}, u32[]{:S(2)}, u32[]{:S(2)}) async-start(bf16[16,40,256]{2,1,0:T(8,128)(2,1)} %pad_maximum_fusion.1), calls=%async_computation | async-start | bytes 655360 | tf_op jit(solution)/shard_map/all_to_all | solution.py:402
  11.9 0.7 constant_dynamic-update-slice_fusion.8
  12.6 1.9 %collective-permute-start.1 = (bf16[1,128,4,128]{3,2,1,0:T(4,128)(2,1)S(1)}, bf16[1,128,4,128]{3,2,1,0:T(4,128)(2,1)S(1)}, u32[]{:S(2)}, u32[]{:S(2)}) collective-permute-start(bf16[1,128,4,128]{3,2,1,0:T(4,128)(2,1)S(1)} %get-tuple-element.18), channel_id=1, source_target_pairs={{0,4},{1,5},{2,6},{3,7},{4,0},{5,1},{6,2},{7,3},{8,12},{9,13},{10,... | collective-permute-start | bytes 393224 | tf_op jit(solution)/shard_map/ppermute | solution.py:379
  14.5 2.4 %collective-permute-start.2 = (bf16[1,128,4,128]{3,2,1,0:T(4,128)(2,1)S(1)}, bf16[1,128,4,128]{3,2,1,0:T(4,128)(2,1)S(1)}, u32[]{:S(2)}, u32[]{:S(2)}) collective-permute-start(bf16[1,128,4,128]{3,2,1,0:T(4,128)(2,1)S(1)} %get-tuple-element.18), channel_id=1, source_target_pairs={{0,8},{1,9},{2,10},{3,11},{4,12},{5,13},{6,14},{7,15},{8,0},{9,1},... | collective-permute-start | bytes 393224 | tf_op jit(solution)/shard_map/ppermute | solution.py:379
  17.6 0.7 dynamic-slice_bitcast_fusion.depth_ref
  18.3 4.8 %collective-permute-done.1 = bf16[1,128,4,128]{3,2,1,0:T(4,128)(2,1)S(1)} collective-permute-done((bf16[1,128,4,128]{3,2,1,0:T(4,128)(2,1)S(1)}, bf16[1,128,4,128]{3,2,1,0:T(4,128)(2,1)S(1)}, u32[]{:S(2)}, u32[]{:S(2)}) %collective-permute-start.1) | collective-permute-done | bytes 131104 | tf_op jit(solution)/shard_map/ppermute | solution.py:379
  23.1 8.4 %collective-permute-done.2 = bf16[1,128,4,128]{3,2,1,0:T(4,128)(2,1)S(1)} collective-permute-done((bf16[1,128,4,128]{3,2,1,0:T(4,128)(2,1)S(1)}, bf16[1,128,4,128]{3,2,1,0:T(4,128)(2,1)S(1)}, u32[]{:S(2)}, u32[]{:S(2)}) %collective-permute-start.2) | collective-permute-done | bytes 131104 | tf_op jit(solution)/shard_map/ppermute | solution.py:379
  31.9 1.5 collective-permute-start.4
  33.5 1.5 collective-permute-start.5
  34.9 0.6 collective-permute-start.6
  35.5 0.7 constant_dynamic-update-slice_fusion.7
  36.2 0.7 constant_dynamic-update-slice_fusion.6
  36.9 0.7 constant_dynamic-update-slice_fusion.5
  38.4 1.0 select_reduce_fusion
  39.4 6.2 %rise.1.packed = bf16[2,512,1024]{2,1,0:T(8,128)(2,1)S(1)} custom-call(bf16[32,40,256]{2,1,0:T(8,128)(2,1)S(1)} %constant_dynamic-update-slice_fusion.mine_ref, s32[1,512]{1,0:T(1,128)S(1)} %bitcast.21, bf16[512,256]{1,0:T(8,128)(2,1)S(1)} %dynamic-slice_bitcast_fusion.1.depth_ref), custom_call_target="tpu_custom_call" | custom-call | flops 20000000000 | bytes 4194304 | tf_op jit(solution)/shard_map/rise/pallas_call | solution.py:428
  45.6 1.3 copy-done.2
  47.1 7.8 %collective-permute-done.5 = bf16[4,128,4,128]{3,2,1,0:T(4,128)(2,1)S(1)} collective-permute-done((bf16[4,128,4,128]{3,2,1,0:T(4,128)(2,1)S(1)}, bf16[4,128,4,128]{3,2,1,0:T(4,128)(2,1)S(1)}, u32[]{:S(2)}, u32[]{:S(2)}) %collective-permute-start.5) | collective-permute-done | bytes 524320 | tf_op jit(solution)/shard_map/ppermute | solution.py:379
  54.9 0.5 broadcast_minimum_fusion
  55.5 0.6 broadcast_minimum_fusion.1.near_ref
  56.1 1.0 constant_dynamic-update-slice_fusion.4
  57.0 1.0 constant_dynamic-update-slice_fusion.3
  58.0 1.0 constant_dynamic-update-slice_fusion.2.volume_ref
  59.0 1.0 broadcast_select_fusion.ys_ref
  60.0 0.8 broadcast_in_dim.55.xs_ref
  60.8 76.8 %planes.1.made_ref = bf16[32,32,256]{2,1,0:T(8,128)(2,1)} custom-call(s32[65]{0:T(128)} %broadcast_minimum_fusion.1.near_ref, s32[65]{0:T(128)} %get-tuple-element.19.close_ref, s32[16]{0:T(128)} %fusion.17.apart_ref, bf16[32,40,256]{2,1,0:T(8,128)(2,1)} %copy-done.1, s32[1,512]{1,0:T(1,128)} %bitcast.26, s32[512,128]{1,0:T(8,128)} %broadcast_in_dim.55.xs_ref, ...), custom_call_target="tpu_custom_call" | custom-call | flops 80000000000 | bytes 8388608 | tf_op jit(solution)/shard_map/planes/pallas_call | solution.py:441
  137.6 1.0 copy-done
  138.6 15.7 %give_back.1 = bf16[16,32,256]{2,1,0:T(8,128)(2,1)S(1)} custom-call(bf16[32,32,256]{2,1,0:T(8,128)(2,1)S(1)} %copy-done), custom_call_target="tpu_custom_call" | custom-call | tf_op jit(solution)/shard_map/give_back/pallas_call | solution.py:465
  154.4 1.0 copy.20
  (42 shorter events, 2.3 us)
Async XLA Ops:
  0.0 17.0 %copy-start.5 = (bf16[2,512,256]{2,1,0:T(8,128)(2,1)S(1)}, bf16[2,512,256]{2,1,0:T(8,128)(2,1)}, u32[]{:S(2)}) copy-start(bf16[2,512,256]{2,1,0:T(8,128)(2,1)} %constant.125.clone) | copy-start | bytes 1572868
  0.0 17.5 %copy-start.4 = (bf16[2,256,512]{2,1,0:T(8,128)(2,1)S(1)}, bf16[2,256,512]{2,1,0:T(8,128)(2,1)}, u32[]{:S(2)}) copy-start(bf16[2,256,512]{2,1,0:T(8,128)(2,1)} %constant.126.clone) | copy-start | bytes 1572868
  0.0 11.9 %copy-start.3 = (f32[128,128,4]{1,2,0:T(4,128)S(1)}, f32[128,128,4]{1,2,0:T(4,128)}, u32[]{:S(2)}) copy-start(f32[128,128,4]{1,2,0:T(4,128)} %param.13) | copy-start | bytes 786436
  3.5 32.7 %all-to-all-start = ((bf16[16,40,256]{2,1,0:T(8,128)(2,1)}), bf16[16,40,256]{2,1,0:T(8,128)(2,1)S(1)}, u32[]{:S(2)}, u32[]{:S(2)}) async-start(bf16[16,40,256]{2,1,0:T(8,128)(2,1)} %pad_maximum_fusion.1), calls=%async_computation | async-start | bytes 655360 | tf_op jit(solution)/shard_map/all_to_all | solution.py:402
  12.6 10.5 %collective-permute-start.1 = (bf16[1,128,4,128]{3,2,1,0:T(4,128)(2,1)S(1)}, bf16[1,128,4,128]{3,2,1,0:T(4,128)(2,1)S(1)}, u32[]{:S(2)}, u32[]{:S(2)}) collective-permute-start(bf16[1,128,4,128]{3,2,1,0:T(4,128)(2,1)S(1)} %get-tuple-element.18), channel_id=1, source_target_pairs={{0,4},{1,5},{2,6},{3,7},{4,0},{5,1},{6,2},{7,3},{8,12},{9,13},{10,... | collective-permute-start | bytes 393224 | tf_op jit(solution)/shard_map/ppermute | solution.py:379
  14.5 16.9 %collective-permute-start.2 = (bf16[1,128,4,128]{3,2,1,0:T(4,128)(2,1)S(1)}, bf16[1,128,4,128]{3,2,1,0:T(4,128)(2,1)S(1)}, u32[]{:S(2)}, u32[]{:S(2)}) collective-permute-start(bf16[1,128,4,128]{3,2,1,0:T(4,128)(2,1)S(1)} %get-tuple-element.18), channel_id=1, source_target_pairs={{0,8},{1,9},{2,10},{3,11},{4,12},{5,13},{6,14},{7,15},{8,0},{9,1},... | collective-permute-start | bytes 393224 | tf_op jit(solution)/shard_map/ppermute | solution.py:379
  16.9 14.6 %collective-permute-start.3 = (bf16[1,128,4,128]{3,2,1,0:T(4,128)(2,1)S(1)}, bf16[1,128,4,128]{3,2,1,0:T(4,128)(2,1)S(1)}, u32[]{:S(2)}, u32[]{:S(2)}) collective-permute-start(bf16[1,128,4,128]{3,2,1,0:T(4,128)(2,1)S(1)} %get-tuple-element.18), channel_id=1, source_target_pairs={{0,12},{1,13},{2,14},{3,15},{4,8},{5,9},{6,10},{7,11},{8,4},{9,5},... | collective-permute-start | bytes 393224 | tf_op jit(solution)/shard_map/ppermute | solution.py:379
  31.9 15.2 %collective-permute-start.4 = (bf16[4,128,4,128]{3,2,1,0:T(4,128)(2,1)S(1)}, bf16[4,128,4,128]{3,2,1,0:T(4,128)(2,1)S(1)}, u32[]{:S(2)}, u32[]{:S(2)}) collective-permute-start(bf16[4,128,4,128]{3,2,1,0:T(4,128)(2,1)S(1)} %pad_maximum_fusion), channel_id=1, source_target_pairs={{0,1},{1,0},{2,3},{3,2},{4,5},{5,4},{6,7},{7,6},{8,9},{9,8},{10,11... | collective-permute-start | bytes 1572872 | tf_op jit(solution)/shard_map/ppermute | solution.py:379
  33.5 21.4 %collective-permute-start.5 = (bf16[4,128,4,128]{3,2,1,0:T(4,128)(2,1)S(1)}, bf16[4,128,4,128]{3,2,1,0:T(4,128)(2,1)S(1)}, u32[]{:S(2)}, u32[]{:S(2)}) collective-permute-start(bf16[4,128,4,128]{3,2,1,0:T(4,128)(2,1)S(1)} %pad_maximum_fusion), channel_id=1, source_target_pairs={{0,2},{1,3},{2,0},{3,1},{4,6},{5,7},{6,4},{7,5},{8,10},{9,11},{10,... | collective-permute-start | bytes 1572872 | tf_op jit(solution)/shard_map/ppermute | solution.py:379
  34.9 20.0 %collective-permute-start.6 = (bf16[4,128,4,128]{3,2,1,0:T(4,128)(2,1)S(1)}, bf16[4,128,4,128]{3,2,1,0:T(4,128)(2,1)S(1)}, u32[]{:S(2)}, u32[]{:S(2)}) collective-permute-start(bf16[4,128,4,128]{3,2,1,0:T(4,128)(2,1)S(1)} %pad_maximum_fusion), channel_id=1, source_target_pairs={{0,3},{1,2},{2,1},{3,0},{4,7},{5,6},{6,5},{7,4},{8,11},{9,10},{10,... | collective-permute-start | bytes 1572872 | tf_op jit(solution)/shard_map/ppermute | solution.py:379
  36.2 1.6 %collective-permute-start = (bf16[16,40,256]{2,1,0:T(8,128)(2,1)S(1)}, bf16[16,40,256]{2,1,0:T(8,128)(2,1)S(1)}, u32[]{:S(2)}, u32[]{:S(2)}) collective-permute-start(bf16[16,40,256]{2,1,0:T(8,128)(2,1)S(1)} %all-to-all-done), channel_id=1, source_target_pairs={{0,16},{16,0},{1,17},{17,1},{2,18},{18,2},{3,19},{19,3},{4,20},{20... | collective-permute-start | bytes 983048 | tf_op jit(solution)/shard_map/ppermute | solution.py:379
  37.9 7.8 %copy-start.1 = (bf16[32,40,256]{2,1,0:T(8,128)(2,1)}, bf16[32,40,256]{2,1,0:T(8,128)(2,1)S(1)}, u32[]{:S(2)}) copy-start(bf16[32,40,256]{2,1,0:T(8,128)(2,1)S(1)} %constant_dynamic-update-slice_fusion.mine_ref) | copy-start | bytes 1966084
  45.6 1.3 copy-start.2
  137.6 1.0 copy-start
